TPU v7x, 512 devices: a whole 4x8x8 slice. The times are simulated.
512 devices in a mesh: batch: 64 (over z, y), cols: 8 (over x, core).
Axes of the slice: x: 4, y: 8, z: 8, core: 2. Of those that a mesh axis runs over, the one named last changes fastest.
Arguments:
- grad_up: float32 [64, 1024, 4096], P('batch', None, 'cols'), may hold values from -1.75 to 1.75
- grad_down: float32 [64, 4096, 1024], P('batch', 'cols'), may hold values from -1.75 to 1.75
- grad_query: float32 [64, 1024, 1024], P('batch', None, 'cols'), may hold values from -1.75 to 1.75
- grad_key: float32 [64, 1024, 1024], P('batch', None, 'cols'), may hold values from -1.75 to 1.75
- grad_value: float32 [64, 1024, 1024], P('batch', None, 'cols'), may hold values from -1.75 to 1.75
- grad_mixed: float32 [64, 1024, 1024], P('batch', 'cols'), may hold values from -1.75 to 1.75
- grad_norm: float32 [64, 1024], P('batch'), may hold values from -16 to 16
- weight_up: float32 [1024, 4096], P('batch', 'cols'), may hold values from -0.1875 to 0.1875
- weight_down: float32 [4096, 1024], P('cols', 'batch'), may hold values from -0.09375 to 0.09375
- weight_query: float32 [1024, 1024], P('batch', 'cols'), may hold values from -0.1875 to 0.1875
- weight_key: float32 [1024, 1024], P('batch', 'cols'), may hold values from -0.1875 to 0.1875
- weight_value: float32 [1024, 1024], P('batch', 'cols'), may hold values from -0.1875 to 0.1875
- weight_mixed: float32 [1024, 1024], P('cols', 'batch'), may hold values from -0.1875 to 0.1875
- weight_norm: float32 [1024], P('batch'), may hold values from 0.25 to 1.75
Outputs:
- copy_up: bfloat16 [1024, 4096], P(None, 'cols')
- copy_down: bfloat16 [4096, 1024], P('cols')
- copy_query: bfloat16 [1024, 1024], P(None, 'cols')
- copy_key: bfloat16 [1024, 1024], P(None, 'cols')
- copy_value: bfloat16 [1024, 1024], P(None, 'cols')
- copy_mixed: bfloat16 [1024, 1024], P('cols')
- copy_norm: bfloat16 [1024], replicated
- new_up: float32 [1024, 4096], P('batch', 'cols')
- new_down: float32 [4096, 1024], P('cols', 'batch')
- new_query: float32 [1024, 1024], P('batch', 'cols')
- new_key: float32 [1024, 1024], P('batch', 'cols')
- new_value: float32 [1024, 1024], P('batch', 'cols')
- new_mixed: float32 [1024, 1024], P('cols', 'batch')
- new_norm: float32 [1024], P('batch')
All inputs are finite; a program needn't handle non-finite values.
Results may differ from a plain program's by a relative error of at most 0.0004.
Values may be sent and summed in bfloat16 or wider, within the bound.
No kernel may reach another device: no remote copies, remote signals or barrier semaphores. Data moves between devices by JAX's collectives and lax.ppermute only.
A program may use at most 64 MiB of HBM per device.

v0:
```python
import jax
import jax.numpy as jnp
from jax import lax
from jax.sharding import PartitionSpec as P

learn_rate = 0.3


def in_blocks(x, dim, count):
    before, after = (x.shape[:dim], x.shape[dim + 1 :])
    return jnp.moveaxis(x.reshape(*before, count, -1, *after), dim, 0)


def one_scatter(arrays, axis, dims):
    count = lax.axis_size(axis)
    parts = [in_blocks(a, dim, count) for a, dim in zip(arrays, dims)]
    lines = jnp.concatenate([b.reshape(count, -1) for b in parts], axis=1)
    extent = max(16, -(-lines.shape[1] // 1024) * 8)
    lines = jnp.pad(lines, ((0, 0), (0, extent * 128 - lines.shape[1]))).reshape(-1, 128)
    flat, at, done = (lax.psum_scatter(lines, axis, tiled=True).reshape(-1), 0, [])
    for b in parts:
        part = b[0]
        done.append(flat[at : at + part.size].reshape(part.shape))
        at += part.size
    return tuple(done)


def rows_first(arrays, axis, dims):
    turned = [jnp.moveaxis(a, dim, 0) for a, dim in zip(arrays, dims)]
    widths = [t[0].size for t in turned]
    both = jnp.concatenate([t.reshape(-1, w) for t, w in zip(turned, widths)], axis=1)
    whole = lax.all_gather(both, axis, axis=0, tiled=True)
    parts = jnp.split(whole, [sum(widths[:k]) for k in range(1, len(widths))], axis=1)
    return tuple(
        (
            jnp.moveaxis(b.reshape(-1, *t.shape[1:]), 0, dim)
            for b, t, dim in zip(parts, turned, dims)
        )
    )


def shards(
    grad_up,
    grad_down,
    grad_query,
    grad_key,
    grad_value,
    grad_mixed,
    grad_norm,
    weight_up,
    weight_down,
    weight_query,
    weight_key,
    weight_value,
    weight_mixed,
    weight_norm,
):
    mean_up, mean_down, mean_query, mean_key, mean_value, mean_mixed, mean_norm = one_scatter(
        (
            grad_up[0],
            grad_down[0],
            grad_query[0],
            grad_key[0],
            grad_value[0],
            grad_mixed[0],
            grad_norm[0],
        ),
        "batch",
        (0, 1, 0, 0, 0, 1, 0),
    )
    mean_rate = lax.axis_size("batch") ** (-0.5)
    mean_up = mean_up * mean_rate
    mean_down = mean_down * mean_rate
    mean_query = mean_query * mean_rate
    mean_key = mean_key * mean_rate
    mean_value = mean_value * mean_rate
    mean_mixed = mean_mixed * mean_rate
    mean_norm = mean_norm * mean_rate
    new_up = weight_up - learn_rate * mean_up
    new_down = weight_down - learn_rate * mean_down
    new_query = weight_query - learn_rate * mean_query
    new_key = weight_key - learn_rate * mean_key
    new_value = weight_value - learn_rate * mean_value
    new_mixed = weight_mixed - learn_rate * mean_mixed
    new_norm = weight_norm - learn_rate * mean_norm
    copy_up, copy_down, copy_query, copy_key, copy_value, copy_mixed, copy_norm = rows_first(
        (
            new_up.astype(jnp.bfloat16),
            new_down.astype(jnp.bfloat16),
            new_query.astype(jnp.bfloat16),
            new_key.astype(jnp.bfloat16),
            new_value.astype(jnp.bfloat16),
            new_mixed.astype(jnp.bfloat16),
            new_norm.astype(jnp.bfloat16),
        ),
        "batch",
        (0, 1, 0, 0, 0, 1, 0),
    )
    return (
        copy_up,
        copy_down,
        copy_query,
        copy_key,
        copy_value,
        copy_mixed,
        copy_norm,
        new_up,
        new_down,
        new_query,
        new_key,
        new_value,
        new_mixed,
        new_norm,
    )


def solution(mesh):
    placed = (
        P("batch", None, "cols"),
        P("batch", "cols", None),
        P("batch", None, "cols"),
        P("batch", None, "cols"),
        P("batch", None, "cols"),
        P("batch", "cols", None),
        P("batch", None),
        P("batch", "cols"),
        P("cols", "batch"),
        P("batch", "cols"),
        P("batch", "cols"),
        P("batch", "cols"),
        P("cols", "batch"),
        P("batch"),
    )
    return jax.shard_map(
        shards,
        mesh=mesh,
        in_specs=placed,
        out_specs=(
            P(None, "cols"),
            P("cols", None),
            P(None, "cols"),
            P(None, "cols"),
            P(None, "cols"),
            P("cols", None),
            P(),
            P("batch", "cols"),
            P("cols", "batch"),
            P("batch", "cols"),
            P("batch", "cols"),
            P("batch", "cols"),
            P("cols", "batch"),
            P("batch"),
        ),
        check_vma=False,
    )
```

profile of v0, /device:TPU:4, one launch (start us, length us, event | category | flops | bytes accessed | tf_op | source)
XLA Modules:
  0.0 343.8 jit_solution(2726753529117511950)
XLA Ops:
  7.2 0.0 all-reduce.4.cloned.1.call-start
  7.2 1.8 reshape_reshape_squeeze.12
  9.0 1.5 constant_dynamic-update-slice_fusion.6
  10.4 1.9 copy.68
  12.4 0.0 copy-start.2
  12.4 0.0 copy-start.3
  12.4 4.2 %copy.69 = f32[64,512,16]{0,2,1:T(8,128)} copy(f32[64,512,16]{1,2,0:T(8,128)S(1)} %bitcast.22) | data formatting | bytes 4194304 | tf_op jit(solution)/shard_map/transpose | solution.py:11
  16.6 2.8 copy.72
  19.4 0.0 copy-done.2
  19.4 0.9 reshape_reshape_squeeze.13
  20.3 0.0 copy-done.3
  20.3 0.9 reshape_reshape_squeeze.14
  21.2 1.9 reshape_reshape_squeeze.15
  23.1 2.0 copy.70
  25.1 1.6 copy.71
  26.7 1.1 copy.73
  27.8 0.5 broadcast.23
  28.4 0.0 copy-done.11
  28.4 0.7 reduce.5
  29.0 0.1 reshape_squeeze.11
  29.1 1.5 constant_dynamic-update-slice_fusion.5
  30.6 1.9 constant_dynamic-update-slice_fusion.4
  32.5 1.9 constant_dynamic-update-slice_fusion.3
  34.4 0.0 copy-done.1
  34.4 0.9 constant_dynamic-update-slice_fusion.2
  35.3 0.0 copy-done
  35.3 0.9 constant_dynamic-update-slice_fusion.1
  36.2 0.6 constant_dynamic-update-slice_fusion
  36.8 6.0 %pad.4 = f32[64,25600]{1,0:T(8,128)} pad(f32[64,24592]{1,0:T(8,128)} %constant_dynamic-update-slice_fusion, f32[]{:T(128)} %constant.8.clone.1), padding=0_0x0_1008 | pad | bytes 12849156 | tf_op jit(solution)/shard_map/jit(_pad)/pad | solution.py:19
  42.8 6.4 %reshape.72 = f32[12800,128]{1,0:T(8,128)} reshape(f32[64,25600]{1,0:T(8,128)} %pad.4) | data formatting | bytes 13107200 | tf_op jit(solution)/shard_map/reshape | solution.py:19
  49.2 0.0 copy-start.8
  49.2 0.0 copy-start.9
  49.2 0.0 copy-start.10
  49.3 0.0 all-reduce.4.cloned.1.call-update
  49.3 0.0 all-gather.2.cloned.1.call-start
  49.3 1.3 dynamic-slice
  51.3 184.5 %all-reduce.4.cloned.1.call-done = f32[12800,128]{1,0:T(8,128)} async-done(((f32[12800,128]{1,0:T(8,128)}), f32[12800,128]{1,0:T(8,128)}) %all-reduce.4.cloned.1.call-update) | async-done | bytes 6553616
  235.7 0.8 dynamic-slice_multiply_fusion
  236.5 0.1 mul.53
  236.6 0.1 copy.74
  236.7 0.7 dynamic-slice_multiply_fusion.2
  237.5 0.1 mul.59
  237.5 0.1 copy.75
  237.6 0.9 dynamic-slice_bitcast_fusion
  238.5 0.0 copy-done.12
  238.5 0.5 convert_bitcast_fusion
  239.0 0.1 copy.76
  239.1 0.0 copy-done.5
  239.1 0.6 constant_dynamic-update-slice_fusion.13
  239.8 0.0 copy-done.6
  239.8 0.6 constant_dynamic-update-slice_fusion.12
  240.4 0.0 copy-done.7
  240.4 1.3 constant_dynamic-update-slice_fusion.11
  241.7 1.3 constant_dynamic-update-slice_fusion.10
  243.0 1.3 constant_dynamic-update-slice_fusion.9
  244.3 0.6 constant_dynamic-update-slice_fusion.8
  244.9 0.6 copy-done.4
  245.6 0.0 all-gather.2.cloned.1.call-update
  245.6 82.8 %all-gather.2.cloned.1.call-done = bf16[1024,1537]{1,0:T(8,128)(2,1)} async-done(((bf16[16,1537]{1,0:T(8,128)(2,1)}), bf16[1024,1537]{1,0:T(8,128)(2,1)}) %all-gather.2.cloned.1.call-update) | async-done | bytes 3147792 | tf_op jit(solution)/shard_map/all_gather | solution.py:32
  328.4 2.7 slice_bitcast_fusion
  331.0 1.3 copy.77
  332.3 2.1 slice_bitcast_fusion.1
  334.4 0.8 copy.78
  335.3 1.7 slice_reduce_fusion
  (13 shorter events, 0.0 us)
Async XLA Ops:
  7.2 228.5 %all-reduce.4.cloned.1.call-start = ((), (), s32[]{:S(2)}) async-start(), calls=%async_computation.1 | async-start | bytes 13107200
  12.4 7.1 %copy-start.2 = (f32[1,1024,128]{2,1,0:T(8,128)S(1)}, f32[1,1024,128]{2,1,0:T(8,128)}, u32[]{:S(2)}) copy-start(f32[1,1024,128]{2,1,0:T(8,128)} %param.16) | copy-start | bytes 1572868
  12.4 7.9 %copy-start.3 = (f32[1,1024,128]{2,1,0:T(8,128)S(1)}, f32[1,1024,128]{2,1,0:T(8,128)}, u32[]{:S(2)}) copy-start(f32[1,1024,128]{2,1,0:T(8,128)} %param.17) | copy-start | bytes 1572868
  16.6 11.8 %copy-start.11 = (f32[1,1024]{1,0:T(1,128)S(1)}, f32[1,1024]{1,0:T(1,128)}, u32[]{:S(2)}) copy-start(f32[1,1024]{1,0:T(1,128)} %param.20) | copy-start | bytes 12292
  27.8 6.6 %copy-start.1 = (f32[64,2048]{1,0:T(8,128)S(1)}, f32[64,2048]{1,0:T(8,128)}, u32[]{:S(2)}) copy-start(f32[64,2048]{1,0:T(8,128)} %reshape_reshape_squeeze.15) | copy-start | bytes 1572868
  27.8 7.5 %copy-start = (f32[64,2048]{1,0:T(8,128)S(1)}, f32[64,2048]{1,0:T(8,128)}, u32[]{:S(2)}) copy-start(f32[64,2048]{1,0:T(8,128)} %copy.73) | copy-start | bytes 1572868
  49.2 189.3 %copy-start.12 = (f32[16]{0:T(128)S(1)}, f32[16]{0:T(128)}, u32[]{:S(2)}) copy-start(f32[16]{0:T(128)} %param.27) | copy-start | bytes 196
  49.2 189.9 %copy-start.5 = (f32[16,512]{1,0:T(8,128)S(1)}, f32[16,512]{1,0:T(8,128)}, u32[]{:S(2)}) copy-start(f32[16,512]{1,0:T(8,128)} %param.21) | copy-start | bytes 98308
  49.2 190.6 %copy-start.6 = (f32[512,16]{0,1:T(8,128)S(1)}, f32[512,16]{0,1:T(8,128)}, u32[]{:S(2)}) copy-start(f32[512,16]{0,1:T(8,128)} %param.22) | copy-start | bytes 98308
  49.2 191.2 %copy-start.7 = (f32[16,128]{1,0:T(8,128)S(1)}, f32[16,128]{1,0:T(8,128)}, u32[]{:S(2)}) copy-start(f32[16,128]{1,0:T(8,128)} %param.23) | copy-start | bytes 24580
  49.2 192.5 %copy-start.8 = (f32[16,128]{1,0:T(8,128)S(1)}, f32[16,128]{1,0:T(8,128)}, u32[]{:S(2)}) copy-start(f32[16,128]{1,0:T(8,128)} %param.24) | copy-start | bytes 24580
  49.2 193.8 %copy-start.9 = (f32[16,128]{1,0:T(8,128)S(1)}, f32[16,128]{1,0:T(8,128)}, u32[]{:S(2)}) copy-start(f32[16,128]{1,0:T(8,128)} %param.25) | copy-start | bytes 24580
  49.2 195.1 %copy-start.10 = (f32[128,16]{0,1:T(8,128)S(1)}, f32[128,16]{0,1:T(8,128)}, u32[]{:S(2)}) copy-start(f32[128,16]{0,1:T(8,128)} %param.26) | copy-start | bytes 24580
  49.3 279.1 %all-gather.2.cloned.1.call-start = ((), (), s32[]{:S(2)}) async-start(), calls=%async_computation | async-start | bytes 3461120 | tf_op jit(solution)/shard_map/all_gather | solution.py:32
  244.9 0.6 copy-start.4
Sparse Core Ops, SparseCore 0:
  49.4 186.2 all-reduce.3
  245.7 82.6 all-gather.1
where the time goes:
time: 345 us; the launch traced here: 344 us
  waiting for transfers between devices  267 us (77%)
  local copies, waits for them, and re-layouts  53.1 us (15%)
  between operations  14.9 us (4%)
  other arithmetic  8.46 us (2%)
    unnamed x3, waiting for transfers between devices  184 us
    all_gather x1, waiting for transfers between devices, rows_first(): whole = lax.all_gather(both, axis, axis=0, tiled=True)  82.8 us
    unnamed x38, local copies, waits for them, and re-layouts  17.1 us
  transfers between devices with their start and end apart: 2, of which 2 were waited for; matrix products, arithmetic and copies ran while one was open for 0% of the time, Pallas kernels for 0%

commit v1 on v0

--- a/solution.py
+++ b/solution.py
@@ -29,7 +29,9 @@
     turned = [jnp.moveaxis(a, dim, 0) for a, dim in zip(arrays, dims)]
     widths = [t[0].size for t in turned]
     both = jnp.concatenate([t.reshape(-1, w) for t, w in zip(turned, widths)], axis=1)
-    whole = lax.all_gather(both, axis, axis=0, tiled=True)
+    whole = jnp.concatenate(
+        lax.all_to_all(jnp.stack([both] * lax.axis_size(axis)), axis, 0, 0), axis=0
+    )
     parts = jnp.split(whole, [sum(widths[:k]) for k in range(1, len(widths))], axis=1)
     return tuple(
         (

time: 345 us -> 349 us (1.012)
  the two profiles are of different devices: /device:TPU:4 before, /device:TPU:24 now
where the time goes in v1:
time: 349 us; the launch traced here: 348 us
  waiting for transfers between devices  184 us (53%)
  blocking collectives  90.9 us (26%)
  local copies, waits for them, and re-layouts  49.2 us (14%)
  between operations  14.8 us (4%)
  other arithmetic  8.46 us (2%)
    unnamed x2, waiting for transfers between devices  184 us
    all_to_all x1, blocking collectives, rows_first(): lax.all_to_all(jnp.stack([both] * lax.axis_size(axis)), axis, 0, 0)  90.9 us
    unnamed x36, local copies, waits for them, and re-layouts  16.5 us
  transfers between devices with their start and end apart: 1, of which 1 were waited for; matrix products, arithmetic and copies ran while one was open for 0% of the time, Pallas kernels for 0%

profile of v1, /device:TPU:24, one launch (start us, length us, event | category | flops | bytes accessed | tf_op | source)
XLA Modules:
  0.0 347.6 jit_solution(3052250319523237695)
XLA Ops:
  7.2 0.0 all-reduce.4.cloned.1.call-start
  7.2 1.8 reshape_reshape_squeeze.12
  9.0 1.5 constant_dynamic-update-slice_fusion.6
  10.5 1.9 copy.70
  12.4 0.0 copy-start.2
  12.5 0.0 copy-start.3
  12.5 4.2 %copy.71 = f32[64,512,16]{0,2,1:T(8,128)} copy(f32[64,512,16]{1,2,0:T(8,128)S(1)} %bitcast.26) | data formatting | bytes 4194304 | tf_op jit(solution)/shard_map/transpose | solution.py:11
  16.7 2.8 copy.74
  19.5 0.0 copy-done.2
  19.5 0.9 reshape_reshape_squeeze.13
  20.4 0.0 copy-done.3
  20.4 0.9 reshape_reshape_squeeze.14
  21.3 1.9 reshape_reshape_squeeze.15
  23.2 2.0 copy.72
  25.3 1.6 copy.73
  26.8 1.1 copy.75
  28.0 0.5 broadcast.25
  28.5 0.0 copy-done.10
  28.5 0.7 reduce.5
  29.1 0.1 reshape_squeeze.11
  29.2 1.5 constant_dynamic-update-slice_fusion.5
  30.7 1.9 constant_dynamic-update-slice_fusion.4
  32.6 1.9 constant_dynamic-update-slice_fusion.3
  34.5 0.0 copy-done.1
  34.5 0.9 constant_dynamic-update-slice_fusion.2
  35.3 0.0 copy-done
  35.3 0.9 constant_dynamic-update-slice_fusion.1
  36.3 0.6 constant_dynamic-update-slice_fusion
  36.9 6.0 %pad.4 = f32[64,25600]{1,0:T(8,128)} pad(f32[64,24592]{1,0:T(8,128)} %constant_dynamic-update-slice_fusion, f32[]{:T(128)} %constant.8.clone.1), padding=0_0x0_1008 | pad | bytes 12849156 | tf_op jit(solution)/shard_map/jit(_pad)/pad | solution.py:19
  42.9 6.4 %reshape.77 = f32[12800,128]{1,0:T(8,128)} reshape(f32[64,25600]{1,0:T(8,128)} %pad.4) | data formatting | bytes 13107200 | tf_op jit(solution)/shard_map/reshape | solution.py:19
  49.3 0.0 copy-start.7
  49.3 0.0 copy-start.8
  49.3 0.0 copy-start.9
  49.3 0.0 all-reduce.4.cloned.1.call-update
  49.3 1.3 dynamic-slice
  51.3 184.2 %all-reduce.4.cloned.1.call-done = f32[12800,128]{1,0:T(8,128)} async-done(((f32[12800,128]{1,0:T(8,128)}), f32[12800,128]{1,0:T(8,128)}) %all-reduce.4.cloned.1.call-update) | async-done | bytes 6553616
  235.4 0.8 dynamic-slice_multiply_fusion
  236.2 0.1 mul.53
  236.4 0.1 copy.76
  236.5 0.7 dynamic-slice_multiply_fusion.2
  237.2 0.1 mul.59
  237.3 0.1 copy.77
  237.3 0.9 dynamic-slice_bitcast_fusion
  238.3 0.0 copy-done.11
  238.3 0.5 convert_bitcast_fusion
  238.8 0.1 copy.78
  238.9 0.0 copy-done.4
  238.9 0.6 constant_dynamic-update-slice_fusion.13
  239.5 0.6 constant_dynamic-update-slice_fusion.12
  240.1 0.0 copy-done.6
  240.1 1.3 constant_dynamic-update-slice_fusion.11
  241.4 0.0 copy-done.7
  241.4 1.3 constant_dynamic-update-slice_fusion.10
  242.7 0.0 copy-done.8
  242.7 1.3 constant_dynamic-update-slice_fusion.9
  244.1 0.0 copy-done.9
  244.1 0.6 constant_dynamic-update-slice_fusion.8
  244.7 0.2 stack.2
  244.9 90.9 %all_to_all.5 = bf16[64,16,1537]{2,1,0:T(8,128)(2,1)S(1)} all-to-all(bf16[64,16,1537]{2,1,0:T(8,128)(2,1)S(1)} %stack.2), channel_id=1, replica_groups=mesh['batch'=64,'cols'=8] {'batch'}, dimensions={0} | all-to-all | bytes 6295552 | tf_op jit(solution)/shard_map/all_to_all | solution.py:33
  335.8 1.1 slice_bitcast_fusion
  336.9 1.0 slice_bitcast_fusion.1
  337.9 0.7 slice_reduce_fusion
  338.6 1.3 copy.79
  339.9 0.8 copy.80
  (10 shorter events, 0.0 us)
Async XLA Ops:
  7.2 228.3 %all-reduce.4.cloned.1.call-start = ((), (), s32[]{:S(2)}) async-start(), calls=%async_computation.1 | async-start | bytes 13107200
  12.4 7.1 %copy-start.2 = (f32[1,1024,128]{2,1,0:T(8,128)S(1)}, f32[1,1024,128]{2,1,0:T(8,128)}, u32[]{:S(2)}) copy-start(f32[1,1024,128]{2,1,0:T(8,128)} %param.16) | copy-start | bytes 1572868
  12.5 8.0 %copy-start.3 = (f32[1,1024,128]{2,1,0:T(8,128)S(1)}, f32[1,1024,128]{2,1,0:T(8,128)}, u32[]{:S(2)}) copy-start(f32[1,1024,128]{2,1,0:T(8,128)} %param.17) | copy-start | bytes 1572868
  16.7 11.8 %copy-start.10 = (f32[1,1024]{1,0:T(1,128)S(1)}, f32[1,1024]{1,0:T(1,128)}, u32[]{:S(2)}) copy-start(f32[1,1024]{1,0:T(1,128)} %param.20) | copy-start | bytes 12292
  28.0 6.5 %copy-start.1 = (f32[64,2048]{1,0:T(8,128)S(1)}, f32[64,2048]{1,0:T(8,128)}, u32[]{:S(2)}) copy-start(f32[64,2048]{1,0:T(8,128)} %reshape_reshape_squeeze.15) | copy-start | bytes 1572868
  28.0 7.4 %copy-start = (f32[64,2048]{1,0:T(8,128)S(1)}, f32[64,2048]{1,0:T(8,128)}, u32[]{:S(2)}) copy-start(f32[64,2048]{1,0:T(8,128)} %copy.75) | copy-start | bytes 1572868
  49.3 189.0 %copy-start.11 = (f32[16]{0:T(128)S(1)}, f32[16]{0:T(128)}, u32[]{:S(2)}) copy-start(f32[16]{0:T(128)} %param.27) | copy-start | bytes 196
  49.3 189.6 %copy-start.4 = (f32[16,512]{1,0:T(8,128)S(1)}, f32[16,512]{1,0:T(8,128)}, u32[]{:S(2)}) copy-start(f32[16,512]{1,0:T(8,128)} %param.21) | copy-start | bytes 98308
  49.3 190.2 %copy-start.5 = (f32[512,16]{0,1:T(8,128)S(1)}, f32[512,16]{0,1:T(8,128)}, u32[]{:S(2)}) copy-start(f32[512,16]{0,1:T(8,128)} %param.22) | copy-start | bytes 98308
  49.3 190.9 %copy-start.6 = (f32[16,128]{1,0:T(8,128)S(1)}, f32[16,128]{1,0:T(8,128)}, u32[]{:S(2)}) copy-start(f32[16,128]{1,0:T(8,128)} %param.23) | copy-start | bytes 24580
  49.3 192.2 %copy-start.7 = (f32[16,128]{1,0:T(8,128)S(1)}, f32[16,128]{1,0:T(8,128)}, u32[]{:S(2)}) copy-start(f32[16,128]{1,0:T(8,128)} %param.24) | copy-start | bytes 24580
  49.3 193.5 %copy-start.8 = (f32[16,128]{1,0:T(8,128)S(1)}, f32[16,128]{1,0:T(8,128)}, u32[]{:S(2)}) copy-start(f32[16,128]{1,0:T(8,128)} %param.25) | copy-start | bytes 24580
  49.3 194.8 %copy-start.9 = (f32[128,16]{0,1:T(8,128)S(1)}, f32[128,16]{0,1:T(8,128)}, u32[]{:S(2)}) copy-start(f32[128,16]{0,1:T(8,128)} %param.26) | copy-start | bytes 24580
Sparse Core Ops, SparseCore 0:
  49.4 185.9 all-reduce.3
